TPU v7x, 512 devices: a whole 4x8x8 slice. The times are simulated.
512 devices in a mesh: dp: 8 (over x, core), expert: 64 (over y, z).
Axes of the slice: x: 4, y: 8, z: 8, core: 2. Of those that a mesh axis runs over, the one named last changes fastest.
Arguments:
- cotangent: bfloat16 [65536, 3584], P(('dp', 'expert')), may hold values from -0.59765625 to 0.59765625
- expert_ids: int32 [65536, 1], P(('dp', 'expert')), may hold values from 0 to 15; in each aligned block of 128 rows (0 to 127, 128 to 255, ...) at most 12 rows name the same one
- route_weights: float32 [65536, 1], P(('dp', 'expert')), may hold values from 0.1 to 1
- gate_pre: bfloat16 [6144, 16384], P('dp', 'expert'), may hold values from -5 to 5
- up_pre: bfloat16 [6144, 16384], P('dp', 'expert'), may hold values from -5 to 5
- down_weight: bfloat16 [3584, 16384], P('dp', 'expert'), may hold values from -0.1875 to 0.1875
Outputs:
- weight_grad: bfloat16 [3584, 16384], P('dp', 'expert')
- gate_grad: bfloat16 [6144, 16384], P('dp', 'expert')
- up_grad: bfloat16 [6144, 16384], P('dp', 'expert')
Inputs may be any that keep to these rules, and one draw needn't show every extreme that they name: `expert_ids`: each token names one expert. Among the tokens of one device, at most 12 name the same expert, and in every draw some expert is named by exactly 12 tokens of some device.
All inputs are finite; a program needn't handle non-finite values.
Results may differ from a plain program's by a relative error of at most 0.013.
Values may be sent and summed in bfloat16 or wider, within the bound.
A program may use at most 64 MiB of HBM per device.

v0:
```python
import functools

import jax
import jax.numpy as jnp
from jax import lax
from jax.experimental import pallas as pl
from jax.experimental.pallas import tpu as pltpu
from jax.sharding import PartitionSpec as P

SPLIT = 4
EARLY = 2
BUILD = 3
LAG = 2


def kernel(
    sizes,
    cot_hbm,
    ids_hbm,
    weights_hbm,
    gate_hbm,
    up_hbm,
    down_hbm,
    wgrad_ref,
    ggrad_ref,
    ugrad_ref,
    cot_ref,
    ids_ref,
    weights_ref,
    gate_ref,
    up_ref,
    down_ref,
    load,
    sendbuf,
    routed,
    cot_in,
    ids_in,
    weights_in,
    up_out,
    up_in,
    upstream,
    slope,
    active,
    product,
    picker,
    scale,
    z_send,
    z_recv,
    y_send,
    y_recv,
    c_send,
    c_recv,
    x_send,
    x_recv,
    i_send,
    i_recv,
    p_send,
    p_recv,
    u_send,
    u_recv,
):
    n, experts, cap, chunks, width, aligned = sizes
    own = chunks // n
    away = chunks - own
    early = min(EARLY, own - 1)
    ahead = min(BUILD, chunks)
    tokens = ids_ref.shape[1]
    dp = lax.axis_index("dp")
    me = lax.axis_index("expert")
    e, lane = me // SPLIT, me % SPLIT
    across = me - lane + (lane + 2) % SPLIT
    beside = me - lane + (lane // 2) * 2 + (lane + 1) % 2
    lane_across = (lane + 2) % SPLIT

    loads = [
        pltpu.make_async_copy(source, to, load.at[i])
        for i, (source, to) in enumerate(
            (
                (cot_hbm, cot_ref),
                (gate_hbm, gate_ref),
                (up_hbm, up_ref),
                (down_hbm, down_ref),
                (ids_hbm, ids_ref),
                (weights_hbm, weights_ref),
            )
        )
    ]
    for i in (4, 5, 0, 1, 2, 3):
        loads[i].start()

    barrier = pltpu.get_barrier_semaphore()

    def greet(target):
        pl.semaphore_signal(
            barrier, inc=1, device_id=target, device_id_type=pl.DeviceIdType.MESH
        )

    for k in range(1, experts):
        greet({"expert": (e + k) % experts * SPLIT + lane})
    greet({"expert": across})
    greet({"expert": beside})
    for k in range(1, n):
        greet({"dp": (dp + k) % n})

    def send(source, to, sent, arrived, device):
        return pltpu.make_async_remote_copy(
            src_ref=source,
            dst_ref=to,
            send_sem=sent,
            recv_sem=arrived,
            device_id=device,
            device_id_type=pl.DeviceIdType.MESH,
        )

    def chunk_at(t):
        late = jnp.where(t < early + away, own - early, -away)
        return t + jnp.where(t < early, 0, late)

    def columns_of(share, j):
        if aligned:
            return cot_ref.at[:, pl.ds(pl.multiple_of((share * own + j) * width, 128), width)]
        return cot_ref.at[share * own + j]

    def cot_copy(i):
        to = (dp - 1 - i // own + n) % n
        return send(columns_of(to, i % own), cot_in.at[i], x_send.at[i], x_recv.at[i], {"dp": to})

    def ids_copy(k):
        return send(
            ids_ref, ids_in.at[k - 1], i_send.at[k - 1, 0], i_recv.at[k - 1, 0], {"dp": (dp - k + n) % n}
        )

    def weights_copy(k):
        return send(
            weights_ref, weights_in.at[k - 1], i_send.at[k - 1, 1], i_recv.at[k - 1, 1], {"dp": (dp - k + n) % n}
        )

    def product_copy(k):
        return send(
            product.at[0], product.at[k], p_send.at[k - 1], p_recv.at[k - 1], {"dp": (dp - k + n) % n}
        )

    def up_copy(i):
        return send(up_out.at[i], up_in.at[i], u_send.at[i], u_recv.at[i], {"dp": (dp + 1 + i) % n})

    def pick(k, ids_row, weight_row):
        shape = (tokens, tokens)
        first = lax.broadcasted_iota(jnp.int32, shape, 0)
        second = lax.broadcasted_iota(jnp.int32, shape, 1)
        names = lax.broadcasted_iota(jnp.int32, (-(-experts // 16) * 16, tokens), 0) == ids_row
        before = jnp.where(first < second, 1.0, 0.0).astype(jnp.bfloat16)
        earlier = jnp.dot(
            jnp.where(names, 1.0, 0.0).astype(jnp.bfloat16), before, preferred_element_type=jnp.float32
        )
        position = jnp.sum(jnp.where(names, earlier, 0.0), axis=0, keepdims=True).astype(jnp.int32)
        target = ids_row * cap + position
        chosen = lax.broadcasted_iota(jnp.int32, (experts * cap, tokens), 0) == target
        picker[k] = jnp.where(chosen, 1.0, 0.0).astype(jnp.bfloat16)
        scale[k] = jnp.sum(jnp.where(chosen, weight_row, 0.0), axis=1, keepdims=True)

    def place(q, k, columns):
        picked = jnp.dot(picker[k], columns, preferred_element_type=jnp.float32)
        rows = (picked * scale[k]).astype(jnp.bfloat16).reshape(experts, cap, width)
        sendbuf[q] = rows
        routed[q, e, lane] = sendbuf[q, e]

    def build(t):
        q = chunk_at(t)

        @pl.when(q < own)
        def _():
            place(q, 0, columns_of(dp, q)[...])

        @pl.when(q >= own)
        def _():
            cot_copy(q - own).wait_recv()
            place(q, q // own, cot_in[q - own])

    def from_source(q, source):
        at = routed.at[q, source, lane]
        return send(at, at, y_send.at[q], y_recv.at[q], {"expert": across})

    def to_expert(t):
        q = chunk_at(t)
        for k in range(1, experts):
            there = (e + k) % experts
            send(
                sendbuf.at[q, there],
                routed.at[q, e, lane],
                z_send.at[q],
                z_recv.at[q],
                {"expert": there * SPLIT + lane},
            ).start()
        from_source(q, e).start()

    def over_y(q):
        at = routed.at[q, :, lane]
        return send(at, at, y_send.at[q], y_recv.at[q], {"expert": across})

    def over_core(q, turn):
        at = routed.at[q, :, lane if turn == 0 else lane_across]
        return send(at, at, c_send.at[q, turn], c_recv.at[q, turn], {"expert": beside})

    def all_but_one(ref_at, sem):
        pltpu.make_async_copy(ref_at, ref_at, sem).wait()

    loads[4].wait()
    loads[5].wait()
    pick(0, ids_ref[...], weights_ref[...])
    loads[0].wait()
    for j in range(early):
        place(j, 0, columns_of(dp, j)[...])
    pl.semaphore_wait(barrier, experts - 1 + 2 + n - 1)
    for k in range(1, n):
        ids_copy(k).start()
        weights_copy(k).start()

    @pl.loop(0, away)
    def _(i):
        cot_copy(i).start()

    for j in range(early):
        to_expert(j)

    rows_all = gate_ref.shape[0]
    piece = rows_all // 8
    loads[1].wait()
    loads[2].wait()

    @pl.loop(0, 8)
    def _(i):
        at = pl.ds(pl.multiple_of(i * piece, 16), piece)
        gate = gate_ref[at, :].astype(jnp.float32)
        up = up_ref[at, :].astype(jnp.float32)
        sig = jax.nn.sigmoid(gate)
        act = gate * sig
        active[at, :] = act
        slope[at, :] = up * sig * (1.0 + gate * (1.0 - sig))
        product[0, at, :] = (act * up).astype(jnp.bfloat16)
        for k in range(n):
            upstream[k, at, :] = jnp.zeros_like(act)

    for k in range(1, n):
        ids_copy(k).wait_recv()
        weights_copy(k).wait_recv()
        pick(k, ids_in[k - 1], weights_in[k - 1])
    for t in range(early, ahead):
        build(t)
    for t in range(early, ahead - 1):
        to_expert(t)
    for k in range(1, n):
        product_copy(k).start()
    loads[3].wait()

    def gradient(j):
        total = jnp.zeros((width, product.shape[2]), jnp.float32)
        for k in range(n):
            rows = routed[k * own + j].reshape(rows_all, width)
            total = total + lax.dot_general(
                rows, product[k], (((0,), (0,)), ((), ())), preferred_element_type=jnp.float32
            )
        wgrad_ref[j] = total.astype(jnp.bfloat16)

    @pl.loop(0, chunks + LAG + 1)
    def _(t):
        @pl.when(t + ahead < chunks)
        def _():
            build(t + ahead)

        @pl.when(t + ahead - 1 < chunks)
        def _():
            to_expert(t + ahead - 1)

        @pl.when(t < chunks)
        def _():
            q = chunk_at(t)
            all_but_one(routed.at[q, pl.ds(0, experts - 1), 0], z_recv.at[q])
            for k in range(1, experts):
                from_source(q, (e + k) % experts).start()
            over_core(q, 0).start()

        @pl.when((t >= LAG) & (t < chunks + LAG))
        def _():
            q = chunk_at(t - LAG)
            over_y(q).wait_recv()
            over_core(q, 1).start()

        @pl.when(t >= LAG + 1)
        def _():
            turn = t - LAG - 1
            q = chunk_at(turn)
            k, j = q // own, q % own
            over_core(q, 0).wait_recv()
            over_core(q, 1).wait_recv()
            rows = routed[q].reshape(rows_all, width)
            upstream[k] += jnp.dot(rows, down_ref[j], preferred_element_type=jnp.float32)

            @pl.when((k >= 1) & (j == own - 1))
            def _():
                up_out[k - 1] = upstream[k].astype(jnp.bfloat16)

            @pl.when(turn == early + away)
            def _():
                for i in range(1, n):
                    product_copy(i).wait_recv()
                for i in range(early):
                    gradient(i)

            @pl.when(turn >= early + away)
            def _():
                gradient(j)

            @pl.when((k >= 1) & (j == own - 1))
            def _():
                up_copy(k - 1).start()

    for k in range(1, n):
        up_copy(k - 1).wait_recv()

    @pl.loop(0, 8)
    def _(i):
        at = pl.ds(pl.multiple_of(i * piece, 16), piece)
        total = upstream[0, at, :]
        for k in range(1, n):
            total = total + up_in[k - 1, at, :].astype(jnp.float32)
        ggrad_ref[at, :] = (total * slope[at, :]).astype(jnp.bfloat16)
        ugrad_ref[at, :] = (total * active[at, :]).astype(jnp.bfloat16)

    @pl.loop(0, chunks)
    def _(q):
        all_but_one(sendbuf.at[q, pl.ds(0, experts - 1)], z_send.at[q])
        over_y(q).wait_send()
        over_core(q, 0).wait_send()
        over_core(q, 1).wait_send()

    @pl.loop(0, away)
    def _(i):
        cot_copy(i).wait_send()

    for k in range(1, n):
        ids_copy(k).wait_send()
        weights_copy(k).wait_send()
        product_copy(k).wait_send()
        up_copy(k - 1).wait_send()


def chunk_width(depth):
    for width in (256, 128):
        if depth % width == 0:
            return width, True
    return depth, False


def per_device(cotangent, expert_ids, route_weights, gate_pre, up_pre, down_weight):
    n = lax.axis_size("dp")
    devices = lax.axis_size("expert")
    experts = devices // SPLIT
    rows, hidden = gate_pre.shape
    capacity = rows // devices
    cap = -(-capacity // 16) * 16
    depth = down_weight.shape[0]
    width, aligned = chunk_width(depth)
    own = depth // width
    chunks = n * own
    away = chunks - own
    if not aligned:
        cotangent = cotangent.reshape(-1, chunks, width).swapaxes(0, 1)

    def widen(a):
        if cap == capacity:
            return a
        a = a.reshape(devices, capacity, hidden)
        return jnp.pad(a, ((0, 0), (0, cap - capacity), (0, 0))).reshape(devices * cap, hidden)

    def narrow(a):
        if cap == capacity:
            return a
        return a.reshape(devices, cap, hidden)[:, :capacity].reshape(rows, hidden)

    padded = devices * cap
    tokens = expert_ids.shape[0]
    half, full = jnp.bfloat16, jnp.float32
    vmem = pl.BlockSpec(memory_space=pltpu.VMEM)
    anywhere = pl.BlockSpec(memory_space=pltpu.HBM)
    dma = pltpu.SemaphoreType.DMA
    weight_grad, gate_grad, up_grad = pl.pallas_call(
        functools.partial(kernel, (n, experts, cap, chunks, width, aligned)),
        out_shape=(
            pltpu.VMEM((own, width, hidden), half),
            pltpu.VMEM((padded, hidden), half),
            pltpu.VMEM((padded, hidden), half),
        ),
        in_specs=[anywhere] * 6,
        out_specs=(vmem, vmem, vmem),
        scratch_shapes=[
            pltpu.VMEM(cotangent.shape, half),
            pltpu.VMEM((1, tokens), jnp.int32),
            pltpu.VMEM((1, tokens), full),
            pltpu.VMEM((padded, hidden), half),
            pltpu.VMEM((padded, hidden), half),
            pltpu.VMEM((own, width, hidden), half),
            dma((6,)),
            pltpu.VMEM((chunks, experts, cap, width), half),
            pltpu.VMEM((chunks, experts, SPLIT, cap, width), half),
            pltpu.VMEM((away, tokens, width), half),
            pltpu.VMEM((n - 1, 1, tokens), jnp.int32),
            pltpu.VMEM((n - 1, 1, tokens), full),
            pltpu.VMEM((n - 1, padded, hidden), half),
            pltpu.VMEM((n - 1, padded, hidden), half),
            pltpu.VMEM((n, padded, hidden), full),
            pltpu.VMEM((padded, hidden), full),
            pltpu.VMEM((padded, hidden), full),
            pltpu.VMEM((n, padded, hidden), half),
            pltpu.VMEM((n, experts * cap, tokens), half),
            pltpu.VMEM((n, experts * cap, 1), full),
            dma((chunks,)),
            dma((chunks,)),
            dma((chunks,)),
            dma((chunks,)),
            dma((chunks, 2)),
            dma((chunks, 2)),
            dma((away,)),
            dma((away,)),
            dma((n - 1, 2)),
            dma((n - 1, 2)),
            dma((n - 1,)),
            dma((n - 1,)),
            dma((n - 1,)),
            dma((n - 1,)),
        ],
        compiler_params=pltpu.CompilerParams(collective_id=0, has_side_effects=True),
    )(
        cotangent,
        expert_ids.reshape(1, -1),
        route_weights.reshape(1, -1),
        widen(gate_pre),
        widen(up_pre),
        down_weight.reshape(own, width, hidden),
    )
    return weight_grad.reshape(depth, hidden), narrow(gate_grad), narrow(up_grad)


def solution(mesh):
    placed = (
        P(("dp", "expert"), None),
        P(("dp", "expert"), None),
        P(("dp", "expert"), None),
        P("dp", "expert"),
        P("dp", "expert"),
        P("dp", "expert"),
    )
    return jax.shard_map(
        per_device,
        mesh=mesh,
        in_specs=placed,
        out_specs=(P("dp", "expert"), P("dp", "expert"), P("dp", "expert")),
        check_vma=False,
    )
```

profile of v0, /device:TPU:1, one launch (start us, length us, event | category | flops | bytes accessed | tf_op | source)
XLA Modules:
  0.0 227.2 jit_solution(5939846623826649702)
XLA Ops:
  0.6 1.1 reshape.48
  1.7 0.0 copy-start.1
  1.7 0.9 pad.7
  2.6 0.2 copy-done.1
  2.8 0.0 copy-start
  2.8 0.1 reshape.50
  2.9 0.9 pad.8
  3.8 0.4 copy-done
  4.2 0.6 copy.9
  4.8 1.3 copy.10
  6.1 218.7 %shard_map.85 = (bf16[1,448,256]{2,1,0:T(8,128)(2,1)S(1)}, bf16[1024,256]{1,0:T(8,128)(2,1)S(1)}, bf16[1024,256]{1,0:T(8,128)(2,1)S(1)}) custom-call(bf16[8,128,448]{2,1,0:T(8,128)(2,1)} %bitcast.15, s32[1,128]{1,0:T(1,128)} %bitcast.20, f32[1,128]{1,0:T(1,128)} %bitcast.21, bf16[1024,256]{1,0:T(8,128)(2,1)} %bitcast.17, bf16[1024,256]{1,0:T(8,128)(2,1)} %bitcast.18, ...), custom_call_target="tpu_custom_call" | custom-call | tf_op jit(solution)/shard_map/pallas_call | solution.py:386
  224.8 0.7 copy.12
  225.5 0.8 reshape.55
  226.3 0.8 reshape.57
Async XLA Ops:
  1.7 1.1 copy-start.1
  2.8 1.4 copy-start
where the time goes:
time: 227 us
  Pallas kernels  219 us (96%)
  local copies, waits for them, and re-layouts  7.81 us (3%)
    pallas_call x1, Pallas kernels, per_device(): pl.pallas_call(functools.partial(kernel, (n, experts, cap, chunks, width,...  219 us

commit v1 on v0

v1 whole, which is shorter than its diff:
```python
import functools

import jax
import jax.numpy as jnp
from jax import lax
from jax.experimental import pallas as pl
from jax.experimental.pallas import tpu as pltpu
from jax.sharding import PartitionSpec as P

LANES = 4
NZ = 8
GROUPS = 4
WIDTH = 128
SUB = 64


def kernel(
    sizes,
    cot_hbm,
    ids_hbm,
    weights_hbm,
    gate_hbm,
    up_hbm,
    down_hbm,
    wgrad_ref,
    ggrad_ref,
    ugrad_ref,
    cot_ref,
    ids_ref,
    weights_ref,
    gate_ref,
    up_ref,
    load,
    blocks,
    scale,
    sendbuf,
    over_y,
    over_z,
    down,
    slope,
    active,
    perm,
    order,
    product,
    product_in,
    products,
    rows,
    upstream,
    up_mine,
    up_out,
    grads,
    grads_in,
    reduced,
    reduced_in,
    kept,
    half_out,
    half_in,
    y_send,
    y_recv,
    z_send,
    z_recv,
    wz_send,
    wz_recv,
    wx_send,
    wx_recv,
    wc_send,
    wc_recv,
    p_send,
    p_recv,
    u_send,
    u_recv,
    g_send,
    g_recv,
    r_send,
    r_recv,
    o_send,
    o_recv,
):
    n, ny, cap, chunks, quarter = sizes
    nx = n // 2
    experts = 2 * ny
    tokens = ids_ref.shape[1]
    hidden = gate_ref.shape[1]
    slab = GROUPS * cap
    zrows = ny * cap
    half, full = jnp.bfloat16, jnp.float32

    dp = lax.axis_index("dp")
    me = lax.axis_index("expert")
    x, core = dp // 2, dp % 2
    y, z = me // NZ, me % NZ
    side = z // LANES
    pair = z // 2
    inner = 2 * pair + pair % 2
    is_inner = z == inner
    near_z = z + 1 - 2 * (z % 2)
    across_z = NZ - 1 - inner
    outer_z = across_z + 1 - 2 * (across_z % 2)
    partner_z = z - z % LANES + (z % LANES + 2) % LANES
    partner_pair = partner_z // 2
    slots = (z, near_z, across_z, outer_z)
    sibling = {"dp": x * 2 + 1 - core}
    near = {"expert": y * NZ + near_z}
    across = {"expert": y * NZ + across_z}
    partner = {"expert": y * NZ + partner_z}
    far_slot = jnp.where(is_inner, 1, 2)

    def at_y(k):
        return {"expert": (y + k) % ny * NZ + z}

    def at_x(k):
        return {"dp": (x + k) % nx * 2 + core}

    mine_rows = pl.ds(chunks * core, chunks)
    loads = [
        pltpu.make_async_copy(source, to, load.at[i])
        for i, (source, to) in enumerate(
            (
                (ids_hbm, ids_ref),
                (weights_hbm, weights_ref),
                (cot_hbm, cot_ref),
                (down_hbm, down.at[0, x, mine_rows]),
                (gate_hbm, gate_ref),
                (up_hbm, up_ref),
            )
        )
    ]
    for copy in loads:
        copy.start()

    barrier = pltpu.get_barrier_semaphore()

    def greet(target):
        pl.semaphore_signal(
            barrier, inc=1, device_id=target, device_id_type=pl.DeviceIdType.MESH
        )

    for k in range(1, ny):
        greet(at_y(k))
    greet(near)
    greet(across)
    greet({"expert": y * NZ + outer_z})
    greet(partner)
    for k in range(1, n):
        greet({"dp": (dp + k) % n})
    greeted = ny - 1 + 4 + n - 1

    def send(source, to, sent, arrived, device):
        pltpu.make_async_remote_copy(
            src_ref=source,
            dst_ref=to,
            send_sem=sent,
            recv_sem=arrived,
            device_id=device,
            device_id_type=pl.DeviceIdType.MESH,
        ).start()

    def await_bytes(ref_at, sem):
        pltpu.make_async_copy(ref_at, ref_at, sem).wait()

    def steps_of(index, step, count):
        total = jnp.zeros_like(index)
        for k in range(1, count):
            total = total + jnp.where(index >= k * step, 1, 0)
        return total

    loads[0].wait()
    loads[1].wait()
    ids_row, weight_row = ids_ref[...], weights_ref[...]
    first = lax.broadcasted_iota(jnp.int32, (tokens, tokens), 0)
    second = lax.broadcasted_iota(jnp.int32, (tokens, tokens), 1)
    names = lax.broadcasted_iota(jnp.int32, (experts, tokens), 0) == ids_row
    before = jnp.where(first < second, 1.0, 0.0).astype(half)
    earlier = jnp.dot(jnp.where(names, 1.0, 0.0).astype(half), before, preferred_element_type=full)
    position = jnp.sum(jnp.where(names, earlier, 0.0), axis=0, keepdims=True).astype(jnp.int32)
    target = ids_row * cap + position
    shape = (experts, slab, tokens)
    inside = lax.broadcasted_iota(jnp.int32, shape, 1)
    group = steps_of(inside, cap, GROUPS)
    slot = lax.broadcasted_iota(jnp.int32, shape, 0) * cap + inside - group * cap
    slot = slot.reshape(experts * slab, tokens)
    group = group.reshape(experts * slab, tokens)
    chosen = slot == target
    scale[...] = jnp.sum(jnp.where(chosen, weight_row, 0.0), axis=1, keepdims=True)
    for g in range(GROUPS):
        blocks[:, g * tokens : (g + 1) * tokens] = jnp.where(chosen & (group == g), 1.0, 0.0).astype(half)

    def pick(j):
        columns = jnp.concatenate(
            [
                cot_ref[:, pl.ds(pl.multiple_of(g * quarter + j * WIDTH, WIDTH), WIDTH)]
                for g in range(GROUPS)
            ],
            axis=0,
        )
        picked = jnp.dot(blocks[...], columns, preferred_element_type=full) * scale[...]
        sendbuf[j] = picked.astype(half).reshape(ny, 2, slab, WIDTH)
        for s in range(2):
            over_y[j, s, y] = sendbuf[j, y, s]

    def send_y(j):
        for k in range(1, ny):
            send(
                sendbuf.at[j, (y + k) % ny], over_y.at[j, :, y], y_send.at[j], y_recv.at[j], at_y(k)
            )

    def down_at(f, k):
        return down.at[f, (x - k + nx) % nx, mine_rows]

    def down_other(f, k):
        return down.at[f, (x - k + nx) % nx, pl.ds(chunks * (1 - core), chunks)]

    def send_down_x(f):
        for k in range(1, nx):
            send(down_at(f, 0), down_at(f, 0), wx_send.at[f, k - 1], wx_recv.at[f, k - 1], at_x(k))

    def send_down_core(f, k):
        send(down_at(f, k), down_at(f, k), wc_send.at[f, k], wc_recv.at[f, k], sibling)

    loads[2].wait()
    pick(0)
    loads[3].wait()
    pl.semaphore_wait(barrier, greeted)
    send(down_at(0, 0), down_at(1, 0), wz_send, wz_recv, partner)
    send_y(0)
    send_down_x(0)
    send_down_core(0, 0)

    @pl.loop(1, chunks)
    def _(j):
        pick(j)
        send_y(j)

    @pl.loop(0, NZ)
    def _(a):
        shape = (zrows, NZ * zrows)
        at = lax.broadcasted_iota(jnp.int32, shape, 0)
        b = steps_of(at, cap, ny)
        source = b * zrows + a * cap + at - b * cap
        hit = lax.broadcasted_iota(jnp.int32, shape, 1) == source
        perm[a] = jnp.where(hit, 1.0, 0.0).astype(half)

    loads[4].wait()
    loads[5].wait()

    @pl.loop(0, NZ)
    def _(i):
        at = pl.ds(pl.multiple_of(i * zrows, 16), zrows)
        gate = gate_ref[at, :].astype(full)
        up = up_ref[at, :].astype(full)
        sig = jax.nn.sigmoid(gate)
        act = gate * sig
        active[at, :] = act
        slope[at, :] = up * sig * (1.0 + gate * (1.0 - sig))
        gate_ref[at, :] = (act * up).astype(half)

    @pl.loop(0, NZ)
    def _(a):
        product[a] = jnp.dot(perm[a], gate_ref[...], preferred_element_type=full).astype(half)

    def halves(p):
        return pl.ds(2 * p, 2)

    theirs = (partner_pair, NZ // 2 - 1 - partner_pair)
    ours = (pair, NZ // 2 - 1 - pair)
    for i in range(2):
        send(
            product.at[halves(theirs[i])],
            product_in.at[halves(theirs[i])],
            p_send.at[i],
            p_recv.at[i],
            partner,
        )
    await_bytes(down_at(1, 0), wz_recv)
    send_down_x(1)
    send_down_core(1, 0)

    spread = (zrows, ny * slab)
    for g in range(GROUPS):
        at = lax.broadcasted_iota(jnp.int32, spread, 0)
        b = steps_of(at, cap, ny)
        source = b * slab + g * cap + at - b * cap
        hit = lax.broadcasted_iota(jnp.int32, spread, 1) == source
        order[g * zrows : (g + 1) * zrows, :] = jnp.where(hit, 1.0, 0.0).astype(half)
    upstream[...] = jnp.zeros_like(upstream)

    def send_z(j):
        await_bytes(over_y.at[j, :, pl.ds(0, ny - 1)], y_recv.at[j])
        send(
            over_y.at[j, 1 - side], over_z.at[j, far_slot], z_send.at[j, 1], z_recv.at[j, far_slot], across
        )
        send(over_y.at[j, side], over_z.at[j, 0], z_send.at[j, 0], z_recv.at[j, 0], near)

    def forward(j):
        @pl.when(is_inner)
        def _():
            for s in (1, 2):
                await_bytes(over_z.at[j, s], z_recv.at[j, s])
                send(over_z.at[j, s], over_z.at[j, s], z_send.at[j, s + 1], z_recv.at[j, s], near)

    def forward_down():
        for f in range(2):
            for k in range(1, nx):
                await_bytes(down_at(f, k), wx_recv.at[f, k - 1])
                send_down_core(f, k)

    def gather_products():
        for i in range(2):
            await_bytes(product_in.at[halves(ours[i])], p_recv.at[i])
        for s in range(4):
            at = slice(s * zrows, (s + 1) * zrows)
            products[at, :hidden] = product[slots[s]]
            products[at, hidden:] = product_in[slots[s]]

    def await_down():
        for f in range(2):
            for k in range(nx):
                await_bytes(down_other(f, k), wc_recv.at[f, k])

    def compute(j):
        await_bytes(over_z.at[j, 0], z_recv.at[j, 0])

        @pl.when(jnp.logical_not(is_inner))
        def _():
            for s in (1, 2):
                await_bytes(over_z.at[j, s], z_recv.at[j, s])

        raw = jnp.concatenate(
            [over_y[j, side].reshape(ny * slab, WIDTH)]
            + [over_z[j, s].reshape(ny * slab, WIDTH) for s in range(3)],
            axis=1,
        )
        sorted_rows = jnp.dot(order[...], raw, preferred_element_type=full).astype(half)
        for s in range(4):
            for g in range(GROUPS):
                rows[s * zrows : (s + 1) * zrows, g * WIDTH : (g + 1) * WIDTH] = sorted_rows[
                    g * zrows : (g + 1) * zrows, s * WIDTH : (s + 1) * WIDTH
                ]
        for f in range(2):
            columns = slice(f * hidden, (f + 1) * hidden)
            grad = lax.dot_general(
                rows[...], products[:, columns], (((0,), (0,)), ((), ())), preferred_element_type=full
            )
            grads[j, :, :, :, columns] = grad.astype(half).reshape(GROUPS, 2, SUB, hidden)
        for k in range(2):
            send(grads.at[j, 2 * k + 1 - core], grads_in.at[j, k], g_send.at[j, k], g_recv.at[j, k], sibling)
        for f in range(2):
            columns = slice(f * hidden, (f + 1) * hidden)
            weights = down[f, :, pl.ds(2 * j, 2)].reshape(GROUPS * WIDTH, hidden)
            upstream[:, columns] += jnp.dot(rows[...], weights, preferred_element_type=full)

    def send_upstream():
        for s in range(4):
            at = slice(s * zrows, (s + 1) * zrows)
            up_mine[slots[s]] = upstream[at, :hidden].astype(half)
            up_out[slots[s]] = upstream[at, hidden:].astype(half)
        for i in range(2):
            send(
                up_out.at[halves(ours[i])], up_mine.at[halves(ours[i])], u_send.at[i], u_recv.at[i], partner
            )

    def reduce(j):
        for k in range(2):
            await_bytes(grads_in.at[j, k], g_recv.at[j, k])
            total = grads[j, 2 * k + core].astype(full) + grads_in[j, k].astype(full)
            reduced[j, k] = total.astype(half)
            to_x = 2 * k + core
            for i in range(2):
                b = 2 * j + i
                to_core = b // chunks
                at = b % chunks
                here = (to_x == x) & (to_core == core)

                @pl.when(here)
                def _():
                    pltpu.make_async_copy(
                        reduced.at[j, k, i], reduced_in.at[x, at], r_recv.at[x, at]
                    ).start()

                @pl.when(jnp.logical_not(here))
                def _():
                    send(
                        reduced.at[j, k, i],
                        reduced_in.at[x, at],
                        r_send.at[j, k, i],
                        r_recv.at[x, at],
                        {"dp": to_x * 2 + to_core},
                    )

    def owned(j, act):
        for i in range(2):
            b = 2 * j + i

            @pl.when(b // chunks == core)
            def _():
                act(b % chunks)

    def combine(at):
        total = jnp.zeros((SUB, 2 * hidden), full)
        for s in range(nx):
            await_bytes(reduced_in.at[s, at], r_recv.at[s, at])
            total = total + reduced_in[s, at].astype(full)
        kept[at] = total[:, :hidden]
        half_out[at] = total[:, hidden:].astype(half)
        send(half_out.at[at], half_in.at[at], o_send.at[at], o_recv.at[at], partner)

    def finish(at):
        await_bytes(half_in.at[at], o_recv.at[at])
        wgrad_ref[at] = (kept[at] + half_in[at].astype(full)).astype(half)

    @pl.loop(0, chunks + 5)
    def _(t):
        @pl.when(t < chunks)
        def _():
            send_z(t)

        @pl.when((t >= 1) & (t < chunks + 1))
        def _():
            forward(t - 1)

        @pl.when(t == 1)
        def _():
            forward_down()
            gather_products()

        @pl.when(t == 2)
        def _():
            await_down()

        @pl.when((t >= 2) & (t < chunks + 2))
        def _():
            compute(t - 2)

        @pl.when((t >= 3) & (t < chunks + 3))
        def _():
            reduce(t - 3)

        @pl.when(t == chunks + 1)
        def _():
            send_upstream()

        @pl.when((t >= 4) & (t < chunks + 4))
        def _():
            owned(t - 4, combine)

        @pl.when(t >= 5)
        def _():
            owned(t - 5, finish)

    for i in range(2):
        await_bytes(up_mine.at[halves(theirs[i])], u_recv.at[i])

    @pl.loop(0, NZ)
    def _(a):
        at = pl.ds(pl.multiple_of(a * zrows, 16), zrows)
        total = jnp.dot(
            perm[a], up_mine[...].reshape(NZ * zrows, hidden), preferred_element_type=full
        )
        ggrad_ref[at, :] = (total * slope[at, :]).astype(half)
        ugrad_ref[at, :] = (total * active[at, :]).astype(half)

    await_bytes(down_at(0, 0), wz_send)
    for i in range(2):
        await_bytes(product.at[halves(theirs[i])], p_send.at[i])
        await_bytes(up_out.at[halves(ours[i])], u_send.at[i])
    for f in range(2):
        for k in range(nx):
            if k:
                await_bytes(down_at(f, 0), wx_send.at[f, k - 1])
            await_bytes(down_at(f, k), wc_send.at[f, k])

    @pl.loop(0, chunks)
    def _(j):
        await_bytes(sendbuf.at[j, pl.ds(0, ny - 1)], y_send.at[j])
        await_bytes(over_y.at[j, side], z_send.at[j, 0])
        await_bytes(over_y.at[j, 1 - side], z_send.at[j, 1])

        @pl.when(is_inner)
        def _():
            for s in (1, 2):
                await_bytes(over_z.at[j, s], z_send.at[j, s + 1])

        for k in range(2):
            await_bytes(grads.at[j, 2 * k + 1 - core], g_send.at[j, k])
            for i in range(2):

                @pl.when((2 * k + core != x) | ((2 * j + i) // chunks != core))
                def _():
                    await_bytes(reduced.at[j, k, i], r_send.at[j, k, i])

        await_bytes(half_out.at[j], o_send.at[j])


def per_device(cotangent, expert_ids, route_weights, gate_pre, up_pre, down_weight):
    n = lax.axis_size("dp")
    devices = lax.axis_size("expert")
    ny = devices // NZ
    rows, hidden = gate_pre.shape
    cap = rows // devices
    tokens, width = cotangent.shape
    depth = down_weight.shape[0]
    quarter = width // GROUPS
    chunks = quarter // WIDTH
    slab = GROUPS * cap
    zrows = ny * cap
    half, full = jnp.bfloat16, jnp.float32
    vmem = pl.BlockSpec(memory_space=pltpu.VMEM)
    anywhere = pl.BlockSpec(memory_space=pltpu.HBM)
    dma = pltpu.SemaphoreType.DMA
    weight_grad, gate_grad, up_grad = pl.pallas_call(
        functools.partial(kernel, (n, ny, cap, chunks, quarter)),
        out_shape=(
            pltpu.VMEM((chunks, SUB, hidden), half),
            pltpu.VMEM((rows, hidden), half),
            pltpu.VMEM((rows, hidden), half),
        ),
        in_specs=[anywhere] * 6,
        out_specs=(vmem, vmem, vmem),
        scratch_shapes=[
            pltpu.VMEM((tokens, width), half),
            pltpu.VMEM((1, tokens), jnp.int32),
            pltpu.VMEM((1, tokens), full),
            pltpu.VMEM((rows, hidden), half),
            pltpu.VMEM((rows, hidden), half),
            dma((6,)),
            pltpu.VMEM((2 * ny * slab, GROUPS * tokens), half),
            pltpu.VMEM((2 * ny * slab, 1), full),
            pltpu.VMEM((chunks, ny, 2, slab, WIDTH), half),
            pltpu.VMEM((chunks, 2, ny, slab, WIDTH), half),
            pltpu.VMEM((chunks, 3, ny, slab, WIDTH), half),
            pltpu.VMEM((2, n // 2, 2 * chunks, SUB, hidden), half),
            pltpu.VMEM((rows, hidden), full),
            pltpu.VMEM((rows, hidden), full),
            pltpu.VMEM((NZ, zrows, rows), half),
            pltpu.VMEM((GROUPS * zrows, ny * slab), half),
            pltpu.VMEM((NZ, zrows, hidden), half),
            pltpu.VMEM((NZ, zrows, hidden), half),
            pltpu.VMEM((4 * zrows, 2 * hidden), half),
            pltpu.VMEM((4 * zrows, GROUPS * WIDTH), half),
            pltpu.VMEM((4 * zrows, 2 * hidden), full),
            pltpu.VMEM((NZ, zrows, hidden), half),
            pltpu.VMEM((NZ, zrows, hidden), half),
            pltpu.VMEM((chunks, GROUPS, 2, SUB, 2 * hidden), half),
            pltpu.VMEM((chunks, 2, 2, SUB, 2 * hidden), half),
            pltpu.VMEM((chunks, 2, 2, SUB, 2 * hidden), half),
            pltpu.VMEM((n // 2, chunks, SUB, 2 * hidden), half),
            pltpu.VMEM((chunks, SUB, hidden), full),
            pltpu.VMEM((chunks, SUB, hidden), half),
            pltpu.VMEM((chunks, SUB, hidden), half),
            dma((chunks,)),
            dma((chunks,)),
            dma((chunks, 4)),
            dma((chunks, 3)),
            dma,
            dma,
            dma((2, n // 2 - 1)),
            dma((2, n // 2 - 1)),
            dma((2, n // 2)),
            dma((2, n // 2)),
            dma((2,)),
            dma((2,)),
            dma((2,)),
            dma((2,)),
            dma((chunks, 2)),
            dma((chunks, 2)),
            dma((chunks, 2, 2)),
            dma((n // 2, chunks)),
            dma((chunks,)),
            dma((chunks,)),
        ],
        compiler_params=pltpu.CompilerParams(collective_id=0, has_side_effects=True),
    )(
        cotangent,
        expert_ids.reshape(1, -1),
        route_weights.reshape(1, -1),
        gate_pre,
        up_pre,
        down_weight.reshape(chunks, SUB, hidden),
    )
    return weight_grad.reshape(depth, hidden), gate_grad, up_grad


def solution(mesh):
    placed = (
        P(("dp", "expert"), None),
        P(("dp", "expert"), None),
        P(("dp", "expert"), None),
        P("dp", "expert"),
        P("dp", "expert"),
        P("dp", "expert"),
    )
    return jax.shard_map(
        per_device,
        mesh=mesh,
        in_specs=placed,
        out_specs=(P("dp", "expert"), P("dp", "expert"), P("dp", "expert")),
        check_vma=False,
    )
```

time: 227 us -> 102 us (0.45)
  Pallas kernels: 219 us -> 98.9 us
  local copies, waits for them, and re-layouts: 7.81 us -> 2.18 us
    pallas_call x1, Pallas kernels: 219 us -> 98.9 us  [per_device(): pl.pallas_call(functools.partial(kernel, (n, ny, cap, chunks, quarter)),...]
    reshape x5 -> x0, local copies, waits for them, and re-layouts: 4.15 us -> none  [the longest x2 1.67 us: narrow(): return a.reshape(devices, cap, hidden)[:, :capacity].reshape(rows, hidden)]
where the time goes in v1:
time: 102 us
  Pallas kernels  98.9 us (97%)
  local copies, waits for them, and re-layouts  2.18 us (2%)
    pallas_call x1, Pallas kernels, per_device(): pl.pallas_call(functools.partial(kernel, (n, ny, cap, chunks, quarter)),...  98.9 us
    unnamed x3, local copies, waits for them, and re-layouts  2.18 us

profile of v1, /device:TPU:1, one launch (start us, length us, event | category | flops | bytes accessed | tf_op | source)
XLA Modules:
  0.0 101.7 jit_solution(12842717578704446906)
XLA Ops:
  0.6 98.9 %shard_map.85 = (bf16[7,64,256]{2,1,0:T(8,128)(2,1)S(1)}, bf16[768,256]{1,0:T(8,128)(2,1)S(1)}, bf16[768,256]{1,0:T(8,128)(2,1)S(1)}) custom-call(bf16[128,3584]{1,0:T(8,128)(2,1)} %cot_hbm.1, s32[1,128]{1,0:T(1,128)} %bitcast.6, f32[1,128]{1,0:T(1,128)} %bitcast.7, bf16[768,256]{1,0:T(8,128)(2,1)} %gate_hbm.1, bf16[768,256]{1,0:T(8,128)(2,1)} %up_hbm.1, ...), custom_call_target="tpu_custom_call" | custom-call | tf_op jit(solution)/shard_map/pallas_call | solution.py:510
  99.5 0.7 copy.12
  100.2 0.7 copy.13
  100.9 0.7 copy.14
